TPU v7x, 32 devices: a whole 2x2x4 slice. The times are simulated.
32 devices in a mesh: cells: 8 (over z, y), grp: 4 (over x, core).
Axes of the slice: x: 2, y: 2, z: 4, core: 2. Of those that a mesh axis runs over, the one named last changes fastest.
Arguments:
- latent_coordinates: float32 [50, 131072], P(None, ('cells', 'grp')), may hold values from -40 to 40
- group_means: float32 [16, 50], replicated, may hold values from -4 to 4
- entropy_scaling: float32 [16], replicated, may hold values from 0.5 to 2
- sample_shrinkage_lambda: float32 [200], replicated, may hold values from 164 to 1310
- sample_population: int32 [200], replicated, may hold values from 1 to 1310, 131072 in all
Outputs:
- corrected: float32 [50, 131072], P(None, ('cells', 'grp'))
- new_centroids: float32 [16, 50], P('cells')
All inputs are finite; a program needn't handle non-finite values.
Results may differ from a plain program's by a relative error of at most 0.0003.
Values sent between devices are 32-bit elements; how exact they have to be, the bound alone decides.
A program may use at most 64 MiB of HBM per device.

v0:
```python
import functools

import jax
import jax.numpy as jnp
from jax import lax
from jax.experimental import pallas as pl
from jax.experimental.pallas import tpu as pltpu
from jax.sharding import PartitionSpec as P

diversity = 2.0
intercept_ridge = 1.0
highest = lax.Precision.HIGHEST


def from_behind(block, axis, distance):
    devices = range(lax.axis_size(axis))
    route = [(i - distance, i) for i in devices if i - distance in devices]
    return lax.ppermute(block, axis, route)


def observation_affinity(latent_coordinates, group_means, entropy_scaling):
    pairwise_dots = jnp.dot(
        group_means, latent_coordinates, precision=highest, preferred_element_type=jnp.float32
    )
    quadratic_lengths = jnp.sum(group_means * group_means, axis=1)
    return (2.0 * pairwise_dots - quadratic_lengths[:, None]) / (2.0 * entropy_scaling[:, None])


def probabilistic_responsibility(group_affinity):
    top = jnp.max(group_affinity, axis=0, keepdims=True)
    raised = jnp.exp(group_affinity - top)
    return raised / jnp.sum(raised, axis=0, keepdims=True)


def batch_parts(moments, ridge):
    mass = moments[:, 0, :]
    sums = moments[:, 1:, :]
    shrink = ridge[None, :] / (mass + ridge[None, :])
    weight = jnp.sum(mass * shrink, axis=1)
    right_side = jnp.sum(sums * shrink[:, None, :], axis=2)
    return (weight, right_side, jnp.sum(mass, axis=1), jnp.sum(sums, axis=2))


def slopes_of(moments, ridge, weight, right_side):
    mass = moments[:, 0, :]
    sums = moments[:, 1:, :]
    intercept = right_side / (intercept_ridge + weight)[:, None]
    return (sums - mass[:, None, :] * intercept[:, :, None]) / (mass + ridge[None, :])[:, None, :]


def body(
    latent_coordinates, group_means, entropy_scaling, sample_shrinkage_lambda, sample_population
):
    local_cells = latent_coordinates.shape[1]
    num_pcs = latent_coordinates.shape[0]
    clusters = group_means.shape[0]
    batches = sample_population.shape[0]
    owned = clusters // lax.axis_size("cells")
    offset = (lax.axis_index("cells") * lax.axis_size("grp") + lax.axis_index("grp")) * local_cells
    batch_ends = jnp.cumsum(sample_population)
    batch_starts = batch_ends - sample_population
    cells_total = jnp.sum(sample_population).astype(jnp.float32)
    position = offset + lax.iota(jnp.int32, local_cells)
    batch_of = jnp.sum((batch_ends[:, None] <= position[None, :]).astype(jnp.int32), axis=0)
    first_batch = batch_of[0]
    last_batch = batch_of[local_cells - 1]
    group_affinity = observation_affinity(latent_coordinates, group_means, entropy_scaling)
    expected_occupancy = probabilistic_responsibility(group_affinity)

    def count_step(batch_id, running):
        in_batch = (batch_of == batch_id).astype(jnp.float32)
        single_observation = jnp.dot(
            expected_occupancy, in_batch, precision=highest, preferred_element_type=jnp.float32
        )
        return lax.dynamic_update_slice(
            running, single_observation[:, None], (jnp.int32(0), batch_id)
        )

    counts = lax.fori_loop(
        first_batch, last_batch + 1, count_step, jnp.zeros((clusters, batches), jnp.float32)
    )
    counts = lax.psum(counts, ("cells", "grp"))
    totals = jnp.sum(counts, axis=1)
    expected = sample_population.astype(jnp.float32)[None, :] * totals[:, None] / cells_total
    penalty = diversity * jnp.log((counts + 1.0) / (expected + 1.0))

    def penalty_step(batch_id, running):
        in_batch = (batch_of == batch_id).astype(jnp.float32)
        column = lax.dynamic_index_in_dim(penalty, batch_id, 1, keepdims=True)
        return running + column * in_batch[None, :]

    cell_penalty = lax.fori_loop(
        first_batch, last_batch + 1, penalty_step, jnp.zeros((clusters, local_cells), jnp.float32)
    )
    assign = probabilistic_responsibility(group_affinity - cell_penalty)
    augmented = jnp.concatenate(
        [jnp.ones((1, local_cells), jnp.float32), latent_coordinates], axis=0
    )

    def moment_step(batch_id, running):
        in_batch = (batch_of == batch_id).astype(jnp.float32)
        contiguous_portion = jnp.einsum(
            "kn,dn->kd", assign * in_batch[None, :], augmented, precision=highest
        )
        return lax.dynamic_update_slice(
            running, contiguous_portion[:, :, None], (jnp.int32(0), jnp.int32(0), batch_id)
        )

    moments = lax.fori_loop(
        first_batch,
        last_batch + 1,
        moment_step,
        jnp.zeros((clusters, num_pcs + 1, batches), jnp.float32),
    )
    devices_flat = lax.axis_size("cells") * lax.axis_size("grp")
    most_cells = 2 * local_cells * devices_flat // batches
    reach = (most_cells - 2) // local_cells + 1
    begins_here = (batch_starts >= offset) & (batch_starts < offset + local_cells)
    owner_mask = begins_here.astype(jnp.float32)
    head_owned = begins_here[first_batch]
    head_column = lax.dynamic_index_in_dim(moments, first_batch, 2, keepdims=False)
    sent_stats = jnp.where(head_owned, 0.0, 1.0) * head_column
    sent_tag = jnp.where(head_owned, 0.0, first_batch.astype(jnp.float32) + 1.0) * jnp.ones(
        (1,), jnp.float32
    )
    completed = moments
    for hop in range(1, reach + 1):
        got_stats, got_tag = from_behind((sent_stats, sent_tag), ("cells", "grp"), -hop)
        got_id = jnp.maximum(got_tag[0].astype(jnp.int32) - 1, 0)
        accept = jnp.where((got_tag[0] > 0.5) & begins_here[got_id], 1.0, 0.0)
        single_observation = (
            lax.dynamic_index_in_dim(completed, got_id, 2, keepdims=False) + accept * got_stats
        )
        completed = lax.dynamic_update_slice(
            completed, single_observation[:, :, None], (jnp.int32(0), jnp.int32(0), got_id)
        )
    completed = completed * owner_mask[None, None, :]
    weight, right_side, mass_total, moment_total = lax.psum(
        batch_parts(completed, sample_shrinkage_lambda), ("cells", "grp")
    )
    coefficients = slopes_of(completed, sample_shrinkage_lambda, weight, right_side)
    every_centroid = moment_total / (1.0 + mass_total)[:, None]
    new_centroids = lax.dynamic_slice_in_dim(
        every_centroid, lax.axis_index("cells") * owned, owned, 0
    )
    tail_owned = begins_here[last_batch]
    tail_column = lax.dynamic_index_in_dim(coefficients, last_batch, 2, keepdims=False)
    tail_send = jnp.where(tail_owned, 1.0, 0.0) * tail_column
    tail_tag = jnp.where(tail_owned, last_batch.astype(jnp.float32) + 1.0, 0.0) * jnp.ones(
        (1,), jnp.float32
    )
    head_fix = jnp.zeros_like(tail_column)
    for hop in range(1, reach + 1):
        got_coef, got_tag = from_behind((tail_send, tail_tag), ("cells", "grp"), hop)
        match = got_tag[0] == first_batch.astype(jnp.float32) + 1.0
        head_fix = jnp.where(match, got_coef, head_fix)
    own_head = lax.dynamic_index_in_dim(coefficients, first_batch, 2, keepdims=False)
    head_final = jnp.where(head_owned, own_head, head_fix)
    coefficients = lax.dynamic_update_slice(
        coefficients, head_final[:, :, None], (jnp.int32(0), jnp.int32(0), first_batch)
    )

    def correct_step(batch_id, running):
        in_batch = (batch_of == batch_id).astype(jnp.float32)
        slope_table = lax.dynamic_index_in_dim(coefficients, batch_id, 2, keepdims=False)
        moved = jnp.einsum("kd,kn->dn", slope_table, assign * in_batch[None, :], precision=highest)
        return running - moved

    corrected = lax.fori_loop(first_batch, last_batch + 1, correct_step, latent_coordinates)
    return (corrected, new_centroids)


SLOTS = 16
MESH = pl.DeviceIdType.MESH
f32 = jnp.float32
bf16 = jnp.bfloat16


def hi_lo(value):
    hi = value.astype(bf16)
    return hi, (value - hi.astype(f32)).astype(bf16)


def nt_dot(a, b):
    return lax.dot_general(a, b, (((1,), (1,)), ((), ())), preferred_element_type=f32)


def nn_dot(a, b):
    return jnp.dot(a, b, preferred_element_type=f32)


def iota(shape, axis):
    return lax.broadcasted_iota(jnp.int32, shape, axis)


def fiota(shape, axis):
    return iota(shape, axis).astype(f32)


def fused_kernel(
    cells_size, grp_size, chunk,
    x_ref, means_ref, entropy_ref, ridge_ref, population_ref,
    out_ref, centroid_ref,
    xs, xcat, scores, mask, zh, zl, send1, recv1, send_a, recv_a, slab1, slab2,
    sem1, sem_a, sem_b, sem_c,
):
    num_pcs, local = x_ref.shape
    clusters = means_ref.shape[0]
    batches = population_ref.shape[1]
    owned = centroid_ref.shape[0]
    rows = SLOTS * clusters
    wide = xs.shape[0]
    devices = cells_size * grp_size
    chunks = local // chunk
    cell_index = lax.axis_index("cells")
    grp_index = lax.axis_index("grp")
    me = cell_index * grp_size + grp_index

    def at(flat):
        return {"cells": flat // grp_size, "grp": lax.rem(flat, grp_size)}

    barrier = pltpu.get_barrier_semaphore()
    for step in range(1, devices):
        pl.semaphore_signal(
            barrier, inc=1, device_id=at(lax.rem(me + step, devices)), device_id_type=MESH
        )

    population = population_ref[...].astype(f32)
    ridge = ridge_ref[...]
    offset = (me * local).astype(f32)
    ends = jnp.sum(
        jnp.where(iota((batches, batches), 1) <= iota((batches, batches), 0), population, 0.0),
        axis=1, keepdims=True,
    )

    def batch_at(position):
        return jnp.sum(jnp.where(ends <= position, 1.0, 0.0), axis=0, keepdims=True)

    first = batch_at(offset)
    last = batch_at(offset + (local - 1.0))
    prev_last = batch_at(offset - 1.0)
    next_first = batch_at(offset + float(local))
    tail_slot = last - first
    from_prev = jnp.where((prev_last == first) & (first * 0.0 + offset > 0.0), 1.0, 0.0)
    from_next = jnp.where(next_first == last, 1.0, 0.0)
    lane = fiota((SLOTS, batches), 1)
    slot = first + fiota((SLOTS, 1), 0)
    slot_start = jnp.sum(jnp.where(lane < slot, population, 0.0), axis=1, keepdims=True)
    slot_size = jnp.sum(jnp.where(lane == slot, population, 0.0), axis=1, keepdims=True)
    slot_end = slot_start + slot_size
    cells_total = jnp.sum(population, axis=1, keepdims=True)
    size_row = jnp.sum(
        jnp.where(iota((SLOTS, SLOTS), 0) == iota((SLOTS, SLOTS), 1), slot_size, 0.0),
        axis=0, keepdims=True,
    )
    row_slot = first + (iota((rows, 1), 0) // clusters).astype(f32)
    row_ridge = jnp.sum(
        jnp.where(fiota((rows, batches), 1) == row_slot, ridge, 0.0), axis=1, keepdims=True
    )
    row_ridge = jnp.where(row_slot < float(batches), row_ridge, 1.0)

    means = means_ref[...]
    lengths = jnp.sum(means * means, axis=1, keepdims=True)
    twice = 2.0 * entropy_ref[...]

    xs[num_pcs - num_pcs % 8 :, :] = jnp.where(
        iota((wide - num_pcs + num_pcs % 8, local), 0) == num_pcs % 8, 1.0, 0.0
    )
    xs[:num_pcs, :] = x_ref[...]

    def scores_step(index, counts):
        at_lanes = pl.ds(pl.multiple_of(index * chunk, chunk), chunk)
        block = xs[:, at_lanes]
        hi, lo = hi_lo(block)
        xcat[:wide, at_lanes] = hi
        xcat[wide:, at_lanes] = lo
        dots = jnp.dot(
            means, block[:num_pcs], precision=highest, preferred_element_type=f32
        )
        affinity = (2.0 * dots - lengths) / twice
        scores[:, at_lanes] = affinity
        prior = probabilistic_responsibility(affinity)
        position = offset + (index * chunk).astype(f32) + fiota((1, chunk), 1)
        inside = jnp.where(
            (position >= slot_start) & (position < slot_end), 1.0, 0.0
        ).astype(bf16)
        mask[:, at_lanes] = inside
        prior_hi, prior_lo = hi_lo(prior)
        return counts + nt_dot(prior_hi, inside) + nt_dot(prior_lo, inside)

    counts = lax.fori_loop(0, chunks, scores_step, jnp.zeros((clusters, SLOTS), f32))

    slot_lane = fiota((clusters, SLOTS), 1)
    total = jnp.sum(counts, axis=1, keepdims=True)
    tail = jnp.sum(jnp.where(slot_lane == tail_slot, counts, 0.0), axis=1, keepdims=True)
    width = send1.shape[2]
    row_lane = iota((clusters, width), 1)
    row_k = iota((clusters, width), 0)
    packed = (
        jnp.where(row_lane == row_k, total, 0.0)
        + jnp.where(row_lane == row_k + clusters, counts[:, :1], 0.0)
        + jnp.where(row_lane == row_k + 2 * clusters, tail, 0.0)
    )
    packed = jnp.sum(packed, axis=0, keepdims=True)
    send1[0] = packed
    pl.semaphore_wait(barrier, devices - 1)
    for step in range(1, devices):
        pltpu.make_async_remote_copy(
            src_ref=send1.at[0], dst_ref=recv1.at[step - 1],
            send_sem=sem1.at[0], recv_sem=sem1.at[1],
            device_id=at(lax.rem(me + step, devices)), device_id_type=MESH,
        ).start()
    pltpu.make_async_copy(recv1, recv1, sem1.at[1]).wait()

    def column(row, part):
        return jnp.sum(
            jnp.where(row_lane == row_k + part * clusters, row, 0.0), axis=1, keepdims=True
        )

    everyone = packed
    for step in range(1, devices):
        everyone = everyone + recv1[step - 1]
    totals = column(everyone, 0)
    head_more = from_prev * column(recv1[0], 2)
    tail_more = from_next * column(recv1[devices - 2], 1)
    counts = (
        counts
        + jnp.where(slot_lane == 0.0, head_more, 0.0)
        + jnp.where(slot_lane == tail_slot, tail_more, 0.0)
    )
    expected = size_row * totals / cells_total
    penalty = diversity * jnp.log((counts + 1.0) / (expected + 1.0))
    pen_hi = penalty.astype(bf16)
    rest = penalty - pen_hi.astype(f32)
    pen_mid, pen_lo = hi_lo(rest)
    pen_cat = jnp.concatenate([pen_hi, pen_mid, pen_lo], axis=0)

    def assign_step(index, moments):
        at_lanes = pl.ds(pl.multiple_of(index * chunk, chunk), chunk)
        inside = mask[:, at_lanes]
        cell_penalty = nn_dot(pen_cat, inside)
        cell_penalty = (
            cell_penalty[:clusters]
            + cell_penalty[clusters : 2 * clusters]
            + cell_penalty[2 * clusters :]
        )
        assign = probabilistic_responsibility(scores[:, at_lanes] - cell_penalty)
        hi, lo = hi_lo(assign)
        for j in range(SLOTS):
            here = inside[j : j + 1, :]
            zh[j * clusters : (j + 1) * clusters, at_lanes] = hi * here
            zl[j * clusters : (j + 1) * clusters, at_lanes] = lo * here
        first_part = nt_dot(zh[:, at_lanes], xcat[:, at_lanes])
        second_part = nt_dot(zl[:, at_lanes], xcat[:wide, at_lanes])
        return moments + first_part[:, :wide] + first_part[:, wide:] + second_part

    moments = lax.fori_loop(0, chunks, assign_step, jnp.zeros((rows, wide), f32))

    def of_slot(array, j):
        return array[j * clusters : (j + 1) * clusters]

    tail_block = jnp.zeros((clusters, wide), f32)
    for j in range(SLOTS):
        tail_block = tail_block + jnp.where(tail_slot == float(j), of_slot(moments, j), 0.0)
    send_a[0] = tail_block
    send_a[1] = of_slot(moments, 0)
    to_next = pltpu.make_async_remote_copy(
        src_ref=send_a.at[0], dst_ref=recv_a.at[0], send_sem=sem_a.at[0], recv_sem=sem_a.at[1],
        device_id=at(lax.rem(me + 1, devices)), device_id_type=MESH,
    )
    to_prev = pltpu.make_async_remote_copy(
        src_ref=send_a.at[1], dst_ref=recv_a.at[1], send_sem=sem_a.at[2], recv_sem=sem_a.at[3],
        device_id=at(lax.rem(me + devices - 1, devices)), device_id_type=MESH,
    )
    to_next.start()
    to_prev.start()
    to_next.wait_recv()
    to_prev.wait_recv()
    head_more = from_prev * recv_a[0]
    tail_more = from_next * recv_a[1]
    full = []
    for j in range(SLOTS):
        block = of_slot(moments, j) + jnp.where(tail_slot == float(j), tail_more, 0.0)
        full.append(block + head_more if j == 0 else block)

    shrunk_sum = jnp.zeros((clusters, wide), f32)
    plain_sum = jnp.zeros((clusters, wide), f32)
    for j in range(SLOTS):
        lam = of_slot(row_ridge, j)
        shrink = lam / (full[j][:, num_pcs : num_pcs + 1] + lam)
        shrunk_sum = shrunk_sum + shrink * of_slot(moments, j)
        plain_sum = plain_sum + of_slot(moments, j)

    def exchange(slab, value, axis, index, size, sem):
        slab[index] = value
        copies = []
        for step in range(1, size):
            copies.append(
                pltpu.make_async_remote_copy(
                    src_ref=slab.at[index], dst_ref=slab.at[index],
                    send_sem=sem.at[0, step], recv_sem=sem.at[1, step],
                    device_id={axis: lax.rem(index + step, size)}, device_id_type=MESH,
                )
            )
        for copy in copies:
            copy.start()
        for copy in copies:
            copy.wait_recv()
        result = slab[0]
        for step in range(1, size):
            result = result + slab[step]
        return result, copies

    part = jnp.concatenate([shrunk_sum, plain_sum], axis=1)
    part, copies_b = exchange(slab1, part, "grp", grp_index, grp_size, sem_b)
    part, copies_c = exchange(slab2, part, "cells", cell_index, cells_size, sem_c)

    shrunk_sum, plain_sum = part[:, :wide], part[:, wide:]
    intercept = shrunk_sum / (intercept_ridge + shrunk_sum[:, num_pcs : num_pcs + 1])
    centroids = plain_sum / (1.0 + plain_sum[:, num_pcs : num_pcs + 1])
    for r in range(owned):
        picked = jnp.where(
            iota((clusters, wide), 0) == cell_index * owned + r, centroids, 0.0
        )
        centroid_ref[r : r + 1, :] = jnp.sum(picked, axis=0, keepdims=True)[:, :num_pcs]

    slopes = []
    for j in range(SLOTS):
        mass = full[j][:, num_pcs : num_pcs + 1]
        slopes.append((full[j] - mass * intercept) / (mass + of_slot(row_ridge, j)))
    slopes = jnp.concatenate(slopes, axis=0).T
    slope_hi, slope_lo = hi_lo(slopes)
    slope_cat = jnp.concatenate([slope_hi, slope_lo], axis=0)

    def correct_step(index, unused):
        at_lanes = pl.ds(pl.multiple_of(index * chunk, chunk), chunk)
        first_part = nn_dot(slope_cat, zh[:, at_lanes])
        second_part = nn_dot(slope_hi, zl[:, at_lanes])
        moved = first_part[:wide] + first_part[wide:] + second_part
        out_ref[:, at_lanes] = (xs[:, at_lanes] - moved)[:num_pcs]
        return unused

    lax.fori_loop(0, chunks, correct_step, 0)

    pltpu.make_async_copy(recv1, recv1, sem1.at[0]).wait()
    to_next.wait_send()
    to_prev.wait_send()
    for copy in copies_b + copies_c:
        copy.wait_send()


def fused(latent_coordinates, group_means, entropy_scaling, ridge, population):
    num_pcs, local = latent_coordinates.shape
    clusters = group_means.shape[0]
    cells_size, grp_size = lax.axis_size("cells"), lax.axis_size("grp")
    devices = cells_size * grp_size
    rows = SLOTS * clusters
    wide = -(-(num_pcs + 1) // 64) * 64
    width = -(-3 * clusters // 128) * 128
    vmem = pl.BlockSpec(memory_space=pltpu.VMEM)
    dma = pltpu.SemaphoreType.DMA
    return pl.pallas_call(
        functools.partial(fused_kernel, cells_size, grp_size, min(local, 512)),
        out_shape=(
            jax.ShapeDtypeStruct((num_pcs, local), f32),
            jax.ShapeDtypeStruct((clusters // cells_size, num_pcs), f32),
        ),
        in_specs=[vmem] * 5,
        out_specs=(vmem, vmem),
        scratch_shapes=[
            pltpu.VMEM((wide, local), f32),
            pltpu.VMEM((2 * wide, local), bf16),
            pltpu.VMEM((clusters, local), f32),
            pltpu.VMEM((SLOTS, local), bf16),
            pltpu.VMEM((rows, local), bf16),
            pltpu.VMEM((rows, local), bf16),
            pltpu.VMEM((1, 1, width), f32),
            pltpu.VMEM((devices - 1, 1, width), f32),
            pltpu.VMEM((2, clusters, wide), f32),
            pltpu.VMEM((2, clusters, wide), f32),
            pltpu.VMEM((grp_size, clusters, 2 * wide), f32),
            pltpu.VMEM((cells_size, clusters, 2 * wide), f32),
            dma((2,)),
            dma((4,)),
            dma((2, grp_size)),
            dma((2, cells_size)),
        ],
        compiler_params=pltpu.CompilerParams(
            collective_id=0, has_side_effects=True, vmem_limit_bytes=40 * 2**20
        ),
    )(
        latent_coordinates, group_means, entropy_scaling[:, None], ridge[None, :],
        population[None, :],
    )


def step(
    latent_coordinates, group_means, entropy_scaling, sample_shrinkage_lambda, sample_population
):
    local = latent_coordinates.shape[1]
    batches = sample_population.shape[0]
    devices = lax.axis_size("cells") * lax.axis_size("grp")
    args = (
        latent_coordinates, group_means, entropy_scaling, sample_shrinkage_lambda,
        sample_population,
    )
    if 2 * local * devices // batches > local:
        return body(*args)
    ends = jnp.cumsum(sample_population)
    crowded = jnp.any(
        ends[SLOTS - 1 : batches - 1] // local == (ends[: batches - SLOTS] - 1) // local
    )
    return lax.cond(crowded, body, fused, *args)


def solution(mesh):
    return jax.shard_map(
        step,
        mesh=mesh,
        in_specs=(P(None, ("cells", "grp")), P(), P(), P(), P()),
        out_specs=(P(None, ("cells", "grp")), P("cells", None)),
        check_vma=False,
    )
```

profile of v0, /device:TPU:0, one launch (start us, length us, event | category | flops | bytes accessed | tf_op | source)
XLA Modules:
  0.0 34.3 jit_solution(17301411192448216511)
XLA Ops:
  0.6 0.0 copy-start
  0.6 0.0 copy-start.3
  0.7 0.0 copy-start.6
  0.7 0.0 copy-start.5
  0.7 0.0 copy-start.4
  0.7 0.7 %copy-done.4 = s32[200]{0:T(256)S(1)} copy-done((s32[200]{0:T(256)S(1)}, s32[200]{0:T(256)}, u32[]{:S(2)}) %copy-start.4) | copy-done | bytes 824
  1.4 0.3 reduce-window.16
  1.7 0.1 slice.40
  1.9 0.1 slice_reduce_fusion.3
  2.0 0.1 add_bitcast_fusion.1
  2.0 0.7 %compare_reduce_fusion = pred[]{:T(512)} fusion(s32[256]{0:T(256)S(1)} %add_bitcast_fusion.1), kind=kLoop, calls=%fused_computation.58 | loop fusion | flops 6071 | bytes 1473 | tf_op jit(solution)/shard_map/reduce_or | solution.py:510
  3.4 0.0 copy-done
  3.4 0.0 copy-done.3
  3.4 0.0 copy-done.6
  3.4 0.0 copy-done.5
  3.5 29.4 %conditional.1 = ((f32[50,4096]{1,0:T(8,128)S(1)}, f32[2,50]{1,0:T(2,128)S(1)})) conditional(s32[]{:T(128)} %convert_element_type.48, (f32[16]{0:T(128)S(1)}, f32[200]{0:T(256)S(1)}, s32[200]{0:T(256)S(1)}, f32[50,4096]{1,0:T(8,128)S(1)}, f32[16,50]{1,0:T(8,128)S(1)}) %tuple.124, (s32[200]{0:T(256)S(1)}, f32[16,50]{1,0:T(8,128)S(1)}, ...), branch_computations={%region_3.4_spmd, %region_4.32_spmd} | conditional | flops 124604752 | bytes 19026172 | solution.py:513
  3.5 0.1 copy.45.entropy_ref
  3.5 0.1 copy.96.x_ref
  3.6 29.0 %branch_0_fun.1 = (f32[50,4096]{1,0:T(8,128)S(1)}, f32[2,50]{1,0:T(2,128)S(1)}) custom-call(f32[50,4096]{1,0:T(8,128)S(1)} %copy.96.x_ref, f32[16,50]{1,0:T(8,128)S(1)} %get-tuple-element.109.means_ref, f32[16,1]{1,0:T(8,128)S(1)} %copy.45.entropy_ref, f32[1,200]{1,0:T(1,128)S(1)} %bitcast.86, s32[1,200]{1,0:T(1,128)S(1)} %bitcast.85), custom_call_target="tpu_custom_call" | custom-call | tf_op jit(solution)/shard_map/cond/branch_0_fun/pallas_call | solution.py:462
  32.8 0.9 %copy.98 = f32[50,4096]{1,0:T(8,128)} copy(f32[50,4096]{1,0:T(8,128)S(1)} %get-tuple-element.517) | data formatting | bytes 1638400
  33.7 0.6 %copy.99 = f32[2,50]{1,0:T(2,128)} copy(f32[2,50]{1,0:T(2,128)S(1)} %get-tuple-element.518) | data formatting | bytes 800
  (2 shorter events, 0.0 us)
Async XLA Ops:
  0.6 2.8 %copy-start = (f32[50,4096]{1,0:T(8,128)S(1)}, f32[50,4096]{1,0:T(8,128)}, u32[]{:S(2)}) copy-start(f32[50,4096]{1,0:T(8,128)} %param.15) | copy-start | bytes 2457604
  0.6 2.8 %copy-start.3 = (f32[16,50]{1,0:T(8,128)S(1)}, f32[16,50]{1,0:T(8,128)}, u32[]{:S(2)}) copy-start(f32[16,50]{1,0:T(8,128)} %param.16) | copy-start | bytes 9604
  0.7 2.8 %copy-start.6 = (f32[16]{0:T(128)S(1)}, f32[16]{0:T(128)}, u32[]{:S(2)}) copy-start(f32[16]{0:T(128)} %param.17) | copy-start | bytes 196
  0.7 2.8 %copy-start.5 = (f32[200]{0:T(256)S(1)}, f32[200]{0:T(256)}, u32[]{:S(2)}) copy-start(f32[200]{0:T(256)} %param.18) | copy-start | bytes 2404
  0.7 0.8 %copy-start.4 = (s32[200]{0:T(256)S(1)}, s32[200]{0:T(256)}, u32[]{:S(2)}) copy-start(s32[200]{0:T(256)} %param.19) | copy-start | bytes 2404
where the time goes:
time: 34.5 us; the launch traced here: 34.3 us
  Pallas kernels  29 us (84%)
  local copies, waits for them, and re-layouts  2.59 us (8%)
  between operations  1.37 us (4%)
  other arithmetic  1.13 us (3%)
    pallas_call x1, Pallas kernels, fused(): pl.pallas_call(functools.partial(fused_kernel, cells_size, grp_size, min(...  29 us
    unnamed x12, local copies, waits for them, and re-layouts  2.25 us
    reduce_or x1, other arithmetic, step(): jnp.any(ends[SLOTS - 1:batches - 1] // local == (ends[:batches - SLOTS] -...  0.71 us

commit v1 on v0

--- a/solution.py
+++ b/solution.py
@@ -201,8 +201,8 @@
     cells_size, grp_size, chunk,
     x_ref, means_ref, entropy_ref, ridge_ref, population_ref,
     out_ref, centroid_ref,
-    xs, xcat, scores, mask, zh, zl, send1, recv1, send_a, recv_a, slab1, slab2,
-    sem1, sem_a, sem_b, sem_c,
+    xs, xt, scores, mask, spread, zh, zl, send1, recv1, send_a, recv_a, slab1, slab2, slab3,
+    sem1, sem_a, sem_b, sem_c, sem_d,
 ):
     num_pcs, local = x_ref.shape
     clusters = means_ref.shape[0]
@@ -271,9 +271,6 @@
     def scores_step(index, counts):
         at_lanes = pl.ds(pl.multiple_of(index * chunk, chunk), chunk)
         block = xs[:, at_lanes]
-        hi, lo = hi_lo(block)
-        xcat[:wide, at_lanes] = hi
-        xcat[wide:, at_lanes] = lo
         dots = jnp.dot(
             means, block[:num_pcs], precision=highest, preferred_element_type=f32
         )
@@ -310,6 +307,19 @@
             send_sem=sem1.at[0], recv_sem=sem1.at[1],
             device_id=at(lax.rem(me + step, devices)), device_id_type=MESH,
         ).start()
+
+    def ready_step(index, unused):
+        at_lanes = pl.ds(pl.multiple_of(index * chunk, chunk), chunk)
+        hi, lo = hi_lo(xs[:, at_lanes].T)
+        xt[at_lanes, :] = jnp.concatenate([hi, lo], axis=1)
+        inside = mask[:, at_lanes]
+        for j in range(SLOTS):
+            spread[j * clusters : (j + 1) * clusters, at_lanes] = jnp.broadcast_to(
+                inside[j : j + 1, :], (clusters, chunk)
+            )
+        return unused
+
+    lax.fori_loop(0, chunks, ready_step, 0)
     pltpu.make_async_copy(recv1, recv1, sem1.at[1]).wait()
 
     def column(row, part):
@@ -347,14 +357,14 @@
         assign = probabilistic_responsibility(scores[:, at_lanes] - cell_penalty)
         hi, lo = hi_lo(assign)
         for j in range(SLOTS):
-            here = inside[j : j + 1, :]
+            here = spread[j * clusters : (j + 1) * clusters, at_lanes]
             zh[j * clusters : (j + 1) * clusters, at_lanes] = hi * here
             zl[j * clusters : (j + 1) * clusters, at_lanes] = lo * here
-        first_part = nt_dot(zh[:, at_lanes], xcat[:, at_lanes])
-        second_part = nt_dot(zl[:, at_lanes], xcat[:wide, at_lanes])
-        return moments + first_part[:, :wide] + first_part[:, wide:] + second_part
-
-    moments = lax.fori_loop(0, chunks, assign_step, jnp.zeros((rows, wide), f32))
+        cells = xt[at_lanes, :]
+        return moments + nn_dot(zh[:, at_lanes], cells) + nn_dot(zl[:, at_lanes], cells)
+
+    moments = lax.fori_loop(0, chunks, assign_step, jnp.zeros((rows, 2 * wide), f32))
+    moments = moments[:, :wide] + moments[:, wide:]
 
     def of_slot(array, j):
         return array[j * clusters : (j + 1) * clusters]
@@ -391,7 +401,7 @@
         shrunk_sum = shrunk_sum + shrink * of_slot(moments, j)
         plain_sum = plain_sum + of_slot(moments, j)
 
-    def exchange(slab, value, axis, index, size, sem):
+    def send(slab, value, axis, index, size, sem):
         slab[index] = value
         copies = []
         for step in range(1, size):
@@ -404,25 +414,23 @@
             )
         for copy in copies:
             copy.start()
+        return copies
+
+    def gathered(slab, size, copies):
         for copy in copies:
             copy.wait_recv()
         result = slab[0]
         for step in range(1, size):
             result = result + slab[step]
-        return result, copies
+        return result
 
     part = jnp.concatenate([shrunk_sum, plain_sum], axis=1)
-    part, copies_b = exchange(slab1, part, "grp", grp_index, grp_size, sem_b)
-    part, copies_c = exchange(slab2, part, "cells", cell_index, cells_size, sem_c)
-
-    shrunk_sum, plain_sum = part[:, :wide], part[:, wide:]
+    copies_b = send(slab1, part, "grp", grp_index, grp_size, sem_b)
+    part = gathered(slab1, grp_size, copies_b)
+    copies_c = send(slab2, part[:, :wide], "cells", cell_index, cells_size, sem_c)
+    copies_d = send(slab3, part[:, wide:], "cells", cell_index, cells_size, sem_d)
+    shrunk_sum = gathered(slab2, cells_size, copies_c)
     intercept = shrunk_sum / (intercept_ridge + shrunk_sum[:, num_pcs : num_pcs + 1])
-    centroids = plain_sum / (1.0 + plain_sum[:, num_pcs : num_pcs + 1])
-    for r in range(owned):
-        picked = jnp.where(
-            iota((clusters, wide), 0) == cell_index * owned + r, centroids, 0.0
-        )
-        centroid_ref[r : r + 1, :] = jnp.sum(picked, axis=0, keepdims=True)[:, :num_pcs]
 
     slopes = []
     for j in range(SLOTS):
@@ -442,10 +450,18 @@
 
     lax.fori_loop(0, chunks, correct_step, 0)
 
+    plain_sum = gathered(slab3, cells_size, copies_d)
+    centroids = plain_sum / (1.0 + plain_sum[:, num_pcs : num_pcs + 1])
+    for r in range(owned):
+        picked = jnp.where(
+            iota((clusters, wide), 0) == cell_index * owned + r, centroids, 0.0
+        )
+        centroid_ref[r : r + 1, :] = jnp.sum(picked, axis=0, keepdims=True)[:, :num_pcs]
+
     pltpu.make_async_copy(recv1, recv1, sem1.at[0]).wait()
     to_next.wait_send()
     to_prev.wait_send()
-    for copy in copies_b + copies_c:
+    for copy in copies_b + copies_c + copies_d:
         copy.wait_send()
 
 
@@ -460,7 +476,7 @@
     vmem = pl.BlockSpec(memory_space=pltpu.VMEM)
     dma = pltpu.SemaphoreType.DMA
     return pl.pallas_call(
-        functools.partial(fused_kernel, cells_size, grp_size, min(local, 512)),
+        functools.partial(fused_kernel, cells_size, grp_size, min(local, 2048)),
         out_shape=(
             jax.ShapeDtypeStruct((num_pcs, local), f32),
             jax.ShapeDtypeStruct((clusters // cells_size, num_pcs), f32),
@@ -469,9 +485,10 @@
         out_specs=(vmem, vmem),
         scratch_shapes=[
             pltpu.VMEM((wide, local), f32),
-            pltpu.VMEM((2 * wide, local), bf16),
+            pltpu.VMEM((local, 2 * wide), bf16),
             pltpu.VMEM((clusters, local), f32),
             pltpu.VMEM((SLOTS, local), bf16),
+            pltpu.VMEM((rows, local), bf16),
             pltpu.VMEM((rows, local), bf16),
             pltpu.VMEM((rows, local), bf16),
             pltpu.VMEM((1, 1, width), f32),
@@ -479,10 +496,12 @@
             pltpu.VMEM((2, clusters, wide), f32),
             pltpu.VMEM((2, clusters, wide), f32),
             pltpu.VMEM((grp_size, clusters, 2 * wide), f32),
-            pltpu.VMEM((cells_size, clusters, 2 * wide), f32),
+            pltpu.VMEM((cells_size, clusters, wide), f32),
+            pltpu.VMEM((cells_size, clusters, wide), f32),
             dma((2,)),
             dma((4,)),
             dma((2, grp_size)),
+            dma((2, cells_size)),
             dma((2, cells_size)),
         ],
         compiler_params=pltpu.CompilerParams(

time: 34.5 us -> 30 us (0.87)
  Pallas kernels: 29 us -> 24.5 us
    pallas_call x1, Pallas kernels: 29 us -> 24.5 us  [fused(): pl.pallas_call(functools.partial(fused_kernel, cells_size, grp_size, min(...]
where the time goes in v1:
time: 30 us; the launch traced here: 29.8 us
  Pallas kernels  24.5 us (82%)
  local copies, waits for them, and re-layouts  2.59 us (9%)
  between operations  1.37 us (5%)
  other arithmetic  1.13 us (4%)
    pallas_call x1, Pallas kernels, fused(): pl.pallas_call(functools.partial(fused_kernel, cells_size, grp_size, min(...  24.5 us
    unnamed x12, local copies, waits for them, and re-layouts  2.25 us
    reduce_or x1, other arithmetic, step(): jnp.any(ends[SLOTS - 1:batches - 1] // local == (ends[:batches - SLOTS] -...  0.71 us

profile of v1, /device:TPU:0, one launch (start us, length us, event | category | flops | bytes accessed | tf_op | source)
XLA Modules:
  0.0 29.8 jit_solution(10301390489480719432)
XLA Ops:
  0.6 0.0 copy-start
  0.6 0.0 copy-start.3
  0.7 0.0 copy-start.6
  0.7 0.0 copy-start.5
  0.7 0.0 copy-start.4
  0.7 0.7 %copy-done.4 = s32[200]{0:T(256)S(1)} copy-done((s32[200]{0:T(256)S(1)}, s32[200]{0:T(256)}, u32[]{:S(2)}) %copy-start.4) | copy-done | bytes 824
  1.4 0.3 %reduce-window.16 = s32[2,128]{1,0:T(2,128)S(1)} reduce-window(s32[2,128]{1,0:T(2,128)S(1)} %pad_bitcast_fusion.1, s32[]{:T(128)} %constant.118.clone.1), window={size=1x128 pad=0_0x127_0}, to_apply=%region_0.0 | reduce-window | flops 32512 | bytes 2052 | tf_op jit(solution)/shard_map/reduce-window.2
  1.7 0.1 slice.40
  1.9 0.1 slice_reduce_fusion.3
  2.0 0.1 add_bitcast_fusion.1
  2.0 0.7 %compare_reduce_fusion = pred[]{:T(512)} fusion(s32[256]{0:T(256)S(1)} %add_bitcast_fusion.1), kind=kLoop, calls=%fused_computation.58 | loop fusion | flops 6071 | bytes 1473 | tf_op jit(solution)/shard_map/reduce_or | solution.py:529
  3.4 0.0 copy-done
  3.4 0.0 copy-done.3
  3.4 0.0 copy-done.6
  3.4 0.0 copy-done.5
  3.5 24.9 %conditional.1 = ((f32[50,4096]{1,0:T(8,128)S(1)}, f32[2,50]{1,0:T(2,128)S(1)})) conditional(s32[]{:T(128)} %convert_element_type.48, (f32[16]{0:T(128)S(1)}, f32[200]{0:T(256)S(1)}, s32[200]{0:T(256)S(1)}, f32[50,4096]{1,0:T(8,128)S(1)}, f32[16,50]{1,0:T(8,128)S(1)}) %tuple.124, (s32[200]{0:T(256)S(1)}, f32[16,50]{1,0:T(8,128)S(1)}, ...), branch_computations={%region_3.4_spmd, %region_4.32_spmd} | conditional | flops 124604752 | bytes 19026172 | solution.py:532
  3.5 0.1 copy.45.entropy_ref
  3.5 0.1 copy.96.x_ref
  3.6 24.5 %branch_0_fun.1 = (f32[50,4096]{1,0:T(8,128)S(1)}, f32[2,50]{1,0:T(2,128)S(1)}) custom-call(f32[50,4096]{1,0:T(8,128)S(1)} %copy.96.x_ref, f32[16,50]{1,0:T(8,128)S(1)} %get-tuple-element.109.means_ref, f32[16,1]{1,0:T(8,128)S(1)} %copy.45.entropy_ref, f32[1,200]{1,0:T(1,128)S(1)} %bitcast.86, s32[1,200]{1,0:T(1,128)S(1)} %bitcast.85), custom_call_target="tpu_custom_call" | custom-call | tf_op jit(solution)/shard_map/cond/branch_0_fun/pallas_call | solution.py:478
  28.3 0.9 %copy.98 = f32[50,4096]{1,0:T(8,128)} copy(f32[50,4096]{1,0:T(8,128)S(1)} %get-tuple-element.517) | data formatting | bytes 1638400
  29.3 0.6 %copy.99 = f32[2,50]{1,0:T(2,128)} copy(f32[2,50]{1,0:T(2,128)S(1)} %get-tuple-element.518) | data formatting | bytes 800
  (2 shorter events, 0.0 us)
Async XLA Ops:
  0.6 2.8 %copy-start = (f32[50,4096]{1,0:T(8,128)S(1)}, f32[50,4096]{1,0:T(8,128)}, u32[]{:S(2)}) copy-start(f32[50,4096]{1,0:T(8,128)} %param.15) | copy-start | bytes 2457604
  0.6 2.8 %copy-start.3 = (f32[16,50]{1,0:T(8,128)S(1)}, f32[16,50]{1,0:T(8,128)}, u32[]{:S(2)}) copy-start(f32[16,50]{1,0:T(8,128)} %param.16) | copy-start | bytes 9604
  0.7 2.8 %copy-start.6 = (f32[16]{0:T(128)S(1)}, f32[16]{0:T(128)}, u32[]{:S(2)}) copy-start(f32[16]{0:T(128)} %param.17) | copy-start | bytes 196
  0.7 2.8 %copy-start.5 = (f32[200]{0:T(256)S(1)}, f32[200]{0:T(256)}, u32[]{:S(2)}) copy-start(f32[200]{0:T(256)} %param.18) | copy-start | bytes 2404
  0.7 0.8 %copy-start.4 = (s32[200]{0:T(256)S(1)}, s32[200]{0:T(256)}, u32[]{:S(2)}) copy-start(s32[200]{0:T(256)} %param.19) | copy-start | bytes 2404
